TPU v7x, 32 devices: a whole 2x2x4 slice. The times are simulated.
32 devices in a mesh: lon: 4 (over y, core), lat: 8 (over z, x).
Axes of the slice: x: 2, y: 2, z: 4, core: 2. Of those that a mesh axis runs over, the one named last changes fastest.
Arguments:
- fields: bfloat16 [20, 16, 1024, 512], P(None, None, 'lat', 'lon'), may hold values from -16 to 16
- area: float32 [1024, 512], P('lat', 'lon'), may hold values from 0.2 to 5
- ocean: int32 [16, 1024, 512], P(None, 'lat', 'lon'), may hold values 0 or 1
- partner: int32 [512], replicated, may hold values from 0 to 511, as said below
- counted: int32 [512], replicated, may hold values from 0 to 1, as said below
Outputs:
- zonal_mean: float32 [20, 16, 1024], replicated
Inputs may be any that keep to these rules, and one draw needn't show every extreme that they name: partner pairs the columns: partner[partner[i]] = i and partner[i] != i. Of each pair i, partner[i] exactly one has counted = 1.
All inputs are finite; a program needn't handle non-finite values. No bound on the sum of `ocean` on one device may be relied on, other than what follows from the above.
Results may differ from a plain program's by a relative error of at most 0.0003.
Values may be sent and summed in bfloat16 or wider, within the bound.
A program may use at most 64 MiB of HBM per device.

v0:
```python
import jax
import jax.numpy as jnp
from jax import lax
from jax.sharding import PartitionSpec as P


def per_device(fields, area, ocean, partner, counted):
    lat_rows = area.shape[0]
    lon_cols = area.shape[1]
    offset = lax.axis_index("lon") * lon_cols
    own_partner = lax.dynamic_slice_in_dim(partner, offset, lon_cols, 0)
    own_counted = lax.dynamic_slice_in_dim(counted, offset, lon_cols, 0)
    on_top = lax.axis_index("lat") == lax.axis_size("lat") - 1
    fold_row = jnp.logical_and(on_top, jnp.arange(lat_rows)[:, None] == lat_rows - 1)
    counted_weight = jnp.where(fold_row, own_counted.astype(jnp.float32)[None, :], jnp.float32(1.0))
    cell_weight = counted_weight * area
    oceanic = ocean.astype(jnp.float32)
    weight = cell_weight[None] * oceanic
    row_weight = jnp.sum(cell_weight[None] * (oceanic + 0.05), axis=-1)
    half_own = 0.5 * weight[:, lat_rows - 1, :]
    whole_half = lax.all_gather(half_own, "lon", axis=1, tiled=True)
    from_partner = jnp.take(whole_half, own_partner, axis=1)
    last_weight = jnp.where(on_top, half_own + from_partner, weight[:, lat_rows - 1, :])
    joined = jnp.concatenate([weight[:, : lat_rows - 1, :], last_weight[:, None, :]], axis=1)
    row_sum = jnp.sum(fields.astype(jnp.float32) * joined[None], axis=-1)
    totals, weight_total = lax.psum((row_sum, row_weight), "lon")
    zonal = totals / weight_total[None]
    return lax.all_gather(zonal, "lat", axis=2, tiled=True)


def solution(mesh):
    in_specs = (P(None, None, "lat", "lon"), P("lat", "lon"), P(None, "lat", "lon"), P(), P())
    out_specs = P()
    return jax.shard_map(
        per_device, mesh=mesh, in_specs=in_specs, out_specs=out_specs, check_vma=False
    )
```

profile of v0, /device:TPU:0, one launch (start us, length us, event | category | flops | bytes accessed | tf_op | source)
XLA Modules:
  0.0 113.5 jit_solution(8200151392524318987)
XLA Ops:
  6.5 0.0 all-reduce.2.cloned.1.call-start
  6.5 0.8 dynamic-slice_convert_fusion
  7.3 0.8 compare_and_fusion
  8.1 0.9 select_multiply_fusion
  9.0 1.6 %multiply_reduce_fusion.1 = (f32[16,128]{1,0:T(8,128)S(1)}, f32[16,128,128]{2,1,0:T(8,128)S(1)}) fusion(s32[16,128,128]{2,1,0:T(8,128)} %param.7, f32[128,128]{1,0:T(8,128)S(1)} %select_multiply_fusion), kind=kLoop, calls=%fused_computation.3 | loop fusion | flops 1308672 | bytes 2170880 | tf_op jit(solution)/shard_map/reduce_sum | solution.py:19
  10.6 6.1 %all-gather = f32[16,1,512]{2,1,0:T(1,128)S(1)} all-gather(f32[16,1,128]{2,1,0:T(1,128)S(1)} %slice_multiply_fusion), channel_id=2, replica_groups=mesh['lon'=4,'lat'=8] {'lon'}, dimensions={2}, use_global_device_ids=true | all-gather | bytes 40960 | tf_op jit(solution)/shard_map/all_gather | solution.py:21
  16.7 0.1 copy.16
  16.9 0.7 gather_fusion
  17.6 0.1 pad_maximum_fusion
  17.7 8.9 %multiply_reduce_fusion = f32[20,16,128]{2,1,0:T(8,128)} fusion(bf16[20,16,128,128]{3,2,1,0:T(8,128)(2,1)} %param.5, f32[16,128,128]{2,1,0:T(8,128)S(1)} %pad_maximum_fusion), kind=kLoop, calls=%fused_computation.1 | loop fusion | flops 15687680 | bytes 11698176 | tf_op jit(solution)/shard_map/reduce_sum | solution.py:25
  26.7 0.0 all-reduce.2.cloned.1.call-update
  26.7 0.0 all-gather.3.cloned.1.call-start
  26.7 0.1 copy.17
  26.8 12.6 %psum.15 = f32[16,128]{0,1:T(8,128)S(1)} all-reduce(f32[16,128]{0,1:T(8,128)S(1)} %copy.17), channel_id=1, replica_groups=mesh['lon'=4,'lat'=8] {'lon'}, use_global_device_ids=true, to_apply=%region_3.4 | all-reduce | flops 2048 | bytes 16384 | tf_op jit(solution)/shard_map/psum | solution.py:26
  39.4 0.1 copy.15
  39.5 21.0 %all-reduce.2.cloned.1.call-done = f32[20,16,128]{2,1,0:T(8,128)} async-done(((f32[20,16,128]{2,1,0:T(8,128)}), f32[20,16,128]{2,1,0:T(8,128)}) %all-reduce.2.cloned.1.call-update) | async-done | bytes 163856 | tf_op jit(solution)/shard_map/psum | solution.py:26
  60.5 1.6 %broadcast_divide_fusion = f32[20,16,128]{2,1,0:T(8,128)} fusion(f32[20,16,128]{2,1,0:T(8,128)} %all-reduce.2.cloned.1.call-done, f32[16,128]{1,0:T(8,128)S(1)} %copy.15), kind=kLoop, calls=%fused_computation.5 | loop fusion | flops 40960 | bytes 335872 | tf_op jit(solution)/shard_map/div | solution.py:27
  62.1 0.0 all-gather.3.cloned.1.call-update
  62.1 42.0 %all-gather.3.cloned.1.call-done = f32[20,16,1024]{2,1,0:T(8,128)} async-done(((f32[20,16,128]{2,1,0:T(8,128)}), f32[20,16,1024]{2,1,0:T(8,128)}) %all-gather.3.cloned.1.call-update) | async-done | bytes 1310736 | tf_op jit(solution)/shard_map/all_gather | solution.py:28
  104.1 2.5 %copy.20 = f32[20,16,1024]{2,1,0:T(8,128)} copy(f32[20,16,1024]{2,1,0:T(8,128)} %all-gather.3.cloned.1.call-done) | data formatting | bytes 2621440
  (5 shorter events, 0.1 us)
Async XLA Ops:
  6.5 54.0 %all-reduce.2.cloned.1.call-start = ((), (), s32[]{:S(2)}) async-start(), calls=%async_computation | async-start | bytes 327680 | tf_op jit(solution)/shard_map/psum | solution.py:26
  26.7 77.4 %all-gather.3.cloned.1.call-start = ((), (), s32[]{:S(2)}) async-start(), calls=%async_computation.1 | async-start | bytes 1474560 | tf_op jit(solution)/shard_map/all_gather | solution.py:28
Sparse Core Ops, SparseCore 0:
  26.8 33.6 all-reduce.1
  62.5 41.5 all-gather.2
where the time goes:
time: 114 us; the launch traced here: 113 us
  waiting for transfers between devices  63.1 us (55%)
  blocking collectives  18.7 us (16%)
  other arithmetic  14.7 us (13%)
  between operations  13.5 us (12%)
  local copies, waits for them, and re-layouts  3.5 us (3%)
    all_gather x1, waiting for transfers between devices, per_device(): return lax.all_gather(zonal, 'lat', axis=2, tiled=True)  42 us
    psum x1, waiting for transfers between devices, per_device(): totals, weight_total = lax.psum((row_sum, row_weight), 'lon')  21 us
    psum x1, blocking collectives, per_device(): totals, weight_total = lax.psum((row_sum, row_weight), 'lon')  12.6 us
    reduce_sum x1, other arithmetic, per_device(): row_sum = jnp.sum(fields.astype(jnp.float32) * joined[None], axis=-1)  8.95 us
    all_gather x1, blocking collectives, per_device(): whole_half = lax.all_gather(half_own, 'lon', axis=1, tiled=True)  6.14 us
    unnamed x2, local copies, waits for them, and re-layouts  2.62 us
  transfers between devices with their start and end apart: 2, of which 2 were waited for; matrix products, arithmetic and copies ran while one was open for 0% of the time, Pallas kernels for 0%

commit v1 on v0

v1 whole, which is shorter than its diff:
```python
import functools

import jax
import jax.numpy as jnp
from jax import lax
from jax.experimental import pallas as pl
from jax.experimental.pallas import tpu as pltpu
from jax.sharding import PartitionSpec as P

MESH = pl.DeviceIdType.MESH
GROUP = 8


def kernel(
    dims, fields, area, ocean, partner, counted, out,
    fv, av, ov, pv, cv, wt, wf, hb, part, recv,
    fsem, isem, hs, hr, ps, pr, zs, zr, x0s, x0r, y1s, y1r, y0s, y0r, x1s, x1r, ws, wr, cs, cr,
):
    n_lat, n_lon, nx, nz, ny, nc = dims
    levels, lat_rows, lon_cols = ocean.shape
    rows = fields.shape[0] // n_lon
    groups = rows // GROUP
    first = (groups + 1) // 2 * GROUP
    band, me = lax.axis_index("lat"), lax.axis_index("lon")
    z, x = band // nx, band % nx
    y, core = me // nc, me % nc
    top = band == n_lat - 1
    targets = [(dy, dc) for dy in range(1, ny) for dc in range(nc)]
    targets += [(0, dc) for dc in range(1, nc)]

    def lon_at(dy, dc):
        return ((y + dy) % ny) * nc + (core + dc) % nc

    def lat_at(dz, dx):
        return ((z + dz) % nz) * nx + (x + dx) % nx

    ins = [
        pltpu.make_async_copy(ocean, ov, isem.at[0]),
        pltpu.make_async_copy(area, av, isem.at[1]),
        pltpu.make_async_copy(partner, pv, isem.at[2]),
        pltpu.make_async_copy(counted, cv, isem.at[3]),
    ]
    for c in ins:
        c.start()

    def load(index):
        at = pl.ds(pl.multiple_of(index * GROUP, GROUP), GROUP)
        return pltpu.make_async_copy(fields.at[at], fv.at[at], fsem.at[index])

    for dy, dc in targets + [(0, 0)]:
        owner = lon_at(dy, dc)

        def begin(g, carry, owner=owner):
            load(owner * groups + g).start()
            return carry

        lax.fori_loop(0, groups, begin, 0)

    barrier = pltpu.get_barrier_semaphore()
    greeted = [(0, 0, dy, dc) for dy, dc in targets]
    greeted += [(dz, 0, 0, 0) for dz in range(1, nz)]
    greeted += [(0, dx, 0, 0) for dx in range(1, nx)]
    for dz, dx, dy, dc in greeted:
        pl.semaphore_signal(
            barrier, inc=1, device_id={"lat": lat_at(dz, dx), "lon": lon_at(dy, dc)}, device_id_type=MESH
        )
    pl.semaphore_wait(barrier, len(greeted))

    for c in ins:
        c.wait()
    own_lanes = pl.ds(pl.multiple_of(me * lon_cols, lon_cols), lon_cols)

    @pl.when(top)
    def _():
        fold_ocean = jnp.concatenate(
            [ov[l, lat_rows - 1 : lat_rows, :] for l in range(levels)], axis=0
        ).astype(jnp.float32)
        fold_cell = cv[:, own_lanes].astype(jnp.float32) * av[lat_rows - 1 : lat_rows, :]
        hb[me] = 0.5 * (fold_cell * fold_ocean)

        def h_copy(k, dy, dc, slot):
            return pltpu.make_async_remote_copy(
                src_ref=hb.at[slot], dst_ref=hb.at[slot], send_sem=hs.at[k], recv_sem=hr.at[k],
                device_id={"lat": band, "lon": lon_at(dy, dc)}, device_id_type=MESH,
            )

        for k, (dy, dc) in enumerate(targets):
            h_copy(k, dy, dc, me).start()
        for k, (dy, dc) in enumerate(targets):
            h_copy(k, dy, dc, lon_at(-dy, -dc)).wait_recv()
        whole = jnp.concatenate([hb[q] for q in range(n_lon)], axis=1)
        columns = lax.broadcasted_iota(jnp.int32, (n_lon * lon_cols, lon_cols), 0)
        chosen = (columns == pv[:, own_lanes]).astype(jnp.float32)
        joined = lax.dot_general(
            whole, chosen, (((1,), (0,)), ((), ())),
            precision=lax.Precision.HIGHEST, preferred_element_type=jnp.float32,
        )
        wf[...] = hb[me] + joined
        for k, (dy, dc) in enumerate(targets):
            h_copy(k, dy, dc, me).wait_send()

    @pl.when(jnp.logical_not(top))
    def _():
        wf[...] = jnp.zeros_like(wf)

    fold = jnp.logical_and(
        lax.broadcasted_iota(jnp.int32, (lat_rows, lon_cols), 0) == lat_rows - 1, top
    )
    cell = jnp.where(fold, cv[:, own_lanes].astype(jnp.float32), 1.0) * av[...]

    def weigh(l, carry):
        sea = ov[l].astype(jnp.float32)
        weight = jnp.where(fold, wf[pl.ds(l, 1), :], cell * sea)
        wt[l] = weight.T
        part[me, pl.ds(rows + l, 1), :] = jnp.sum((cell * (sea + 0.05)).T, axis=0, keepdims=True)
        return carry

    lax.fori_loop(0, levels, weigh, 0)
    for dy, dc in targets:
        part[lon_at(dy, dc), rows:, :] = part[me, rows:, :]

    def p_copy(k, dy, dc, src, dst):
        return pltpu.make_async_remote_copy(
            src_ref=part.at[src], dst_ref=recv.at[dst], send_sem=ps.at[k], recv_sem=pr.at[k],
            device_id={"lat": band, "lon": lon_at(dy, dc)}, device_id_type=MESH,
        )

    for k, (dy, dc) in enumerate(targets + [(0, 0)]):
        owner = lon_at(dy, dc)

        def reduce(g, carry, owner=owner):
            index = owner * groups + g
            load(index).wait()
            base = pl.multiple_of((index * GROUP) % levels, GROUP)
            sums = []
            for r in range(GROUP):
                turned = fv[index * GROUP + r].T.astype(jnp.float32)
                sums.append(jnp.sum(turned * wt[base + r], axis=0, keepdims=True))
            part[owner, pl.ds(pl.multiple_of(g * GROUP, GROUP), GROUP), :] = jnp.concatenate(sums, axis=0)
            return carry

        lax.fori_loop(0, groups, reduce, 0)
        if k < len(targets):
            p_copy(k, dy, dc, owner, me).start()

    for k, (dy, dc) in enumerate(targets):
        p_copy(k, dy, dc, me, lon_at(-dy, -dc)).wait_recv()

    slots = [lon_at(dy, dc) for dy, dc in targets]
    total_weight = part[me, rows:, :]
    for s in slots:
        total_weight += recv[s, rows:, :]
    part[me, rows:, :] = total_weight

    def region(dz, dx, dy, dc, half):
        start, size = ((0, rows), (0, first), (first, rows - first))[half]
        return out.at[
            pl.ds(pl.multiple_of(lon_at(dy, dc) * rows + start, GROUP), size),
            pl.ds(pl.multiple_of(lat_at(dz, dx) * lat_rows, lat_rows), lat_rows),
        ]

    own_band = pl.ds(pl.multiple_of(band * lat_rows, lat_rows), lat_rows)
    for g in range(groups):
        at = slice(g * GROUP, (g + 1) * GROUP)
        total = part[me, at, :]
        for s in slots:
            total += recv[s, at, :]
        index = me * groups + g
        base = pl.multiple_of((index * GROUP) % levels, GROUP)
        out[pl.ds(pl.multiple_of(index * GROUP, GROUP), GROUP), own_band] = (
            total / part[me, pl.ds(rows + base, GROUP), :]
        )

    sent = []

    def move(block, half, send, receive, to):
        c = pltpu.make_async_remote_copy(
            src_ref=region(*block, half), dst_ref=region(*block, half), send_sem=send, recv_sem=receive,
            device_id={"lat": lat_at(to[0], to[1]), "lon": lon_at(to[2], to[3])}, device_id_type=MESH,
        )
        return c

    def send(*a):
        c = move(*a)
        c.start()
        sent.append(c)

    handed = []

    def hand(block, half):
        for dc in range(1, nc):
            k = len(handed)
            send(block, half, cs.at[k], cr.at[k], (0, 0, 0, dc))
            handed.append((block[:3] + (-dc,), half, k, dc))

    order = sorted(range(1, nz), key=lambda d: min(d, nz - d))
    for d in order:
        send((0, 0, 0, 0), 0, zs.at[d], zr.at[d], (d, 0, 0, 0))
    for d in [0] + order:
        block = (-d, 0, 0, 0)
        if d:
            move(block, 0, zs.at[d], zr.at[d], (d, 0, 0, 0)).wait_recv()
        for e in range(1, nx):
            send(block, 0, x0s.at[d, e], x0r.at[d, e], (0, e, 0, 0))
        for e in range(1, ny):
            send(block, 0, y1s.at[d, e], y1r.at[d, e], (0, 0, e, 0))
        hand(block, 0)
    for d in [0] + order:
        for e in range(1, nx):
            block = (-d, -e, 0, 0)
            move(block, 0, x0s.at[d, e], x0r.at[d, e], (0, e, 0, 0)).wait_recv()
            for k in range(1, ny):
                send(block, 1, y0s.at[d, e, k], y0r.at[d, e, k], (0, 0, k, 0))
            hand(block, 0)
        for e in range(1, ny):
            block = (-d, 0, -e, 0)
            move(block, 0, y1s.at[d, e], y1r.at[d, e], (0, 0, e, 0)).wait_recv()
            for k in range(1, nx):
                send(block, 2, x1s.at[d, e, k], x1r.at[d, e, k], (0, k, 0, 0))
            hand(block, 0)
    for d in [0] + order:
        for e in range(1, nx):
            for k in range(1, ny):
                block = (-d, -e, -k, 0)
                move(block, 1, y0s.at[d, e, k], y0r.at[d, e, k], (0, 0, k, 0)).wait_recv()
                hand(block, 1)
        for e in range(1, ny):
            for k in range(1, nx):
                block = (-d, -k, -e, 0)
                move(block, 2, x1s.at[d, e, k], x1r.at[d, e, k], (0, k, 0, 0)).wait_recv()
                hand(block, 2)
    for block, half, k, dc in handed:
        move(block, half, cs.at[k], cr.at[k], (0, 0, 0, dc)).wait_recv()
    for c in sent:
        c.wait_send()
    for k, (dy, dc) in enumerate(targets):
        p_copy(k, dy, dc, lon_at(dy, dc), me).wait_send()


def per_device(dims, fields, area, ocean, partner, counted):
    n_lat, n_lon, nx, nz, ny, nc = dims
    count, levels, lat_rows, lon_cols = fields.shape
    total = count * levels
    rows = total // n_lon
    hands = nz * (1 + (nx - 1) + (ny - 1) + 2 * (nx - 1) * (ny - 1)) * max(nc - 1, 1)
    dma = pltpu.SemaphoreType.DMA
    any_space = pl.BlockSpec(memory_space=pl.ANY)
    zonal = pl.pallas_call(
        functools.partial(kernel, dims),
        out_shape=jax.ShapeDtypeStruct((total, n_lat * lat_rows), jnp.float32),
        in_specs=[any_space] * 5,
        out_specs=pl.BlockSpec(memory_space=pltpu.VMEM),
        scratch_shapes=[
            pltpu.VMEM((total, lat_rows, lon_cols), fields.dtype),
            pltpu.VMEM((lat_rows, lon_cols), jnp.float32),
            pltpu.VMEM((levels, lat_rows, lon_cols), jnp.int32),
            pltpu.VMEM((1, n_lon * lon_cols), jnp.int32),
            pltpu.VMEM((1, n_lon * lon_cols), jnp.int32),
            pltpu.VMEM((levels, lon_cols, lat_rows), jnp.float32),
            pltpu.VMEM((levels, lon_cols), jnp.float32),
            pltpu.VMEM((n_lon, levels, lon_cols), jnp.float32),
            pltpu.VMEM((n_lon, rows + levels, lat_rows), jnp.float32),
            pltpu.VMEM((n_lon, rows + levels, lat_rows), jnp.float32),
            dma((total // GROUP,)),
            dma((4,)),
            dma((n_lon,)), dma((n_lon,)),
            dma((n_lon,)), dma((n_lon,)),
            dma((nz,)), dma((nz,)),
            dma((nz, nx)), dma((nz, nx)),
            dma((nz, ny)), dma((nz, ny)),
            dma((nz, nx, ny)), dma((nz, nx, ny)),
            dma((nz, ny, nx)), dma((nz, ny, nx)),
            dma((1,)), dma((1,)),
            dma((hands,)), dma((hands,)),
        ],
        compiler_params=pltpu.CompilerParams(collective_id=0, has_side_effects=True),
    )(
        fields.reshape(total, lat_rows, lon_cols), area, ocean,
        partner.reshape(1, -1), counted.reshape(1, -1),
    )
    return zonal.reshape(count, levels, n_lat * lat_rows)


def solution(mesh):
    n_lat, n_lon = mesh.shape["lat"], mesh.shape["lon"]
    nc = 2 if n_lon % 2 == 0 else 1
    ny = n_lon // nc
    nx = ny if n_lat % ny == 0 else 1
    dims = (n_lat, n_lon, nx, n_lat // nx, ny, nc)
    in_specs = (P(None, None, "lat", "lon"), P("lat", "lon"), P(None, "lat", "lon"), P(), P())
    return jax.shard_map(
        functools.partial(per_device, dims), mesh=mesh, in_specs=in_specs, out_specs=P(), check_vma=False
    )
```

time: 114 us -> 34 us (0.30)
  waiting for transfers between devices: 63.1 us -> 0 us
  Pallas kernels: 0 us -> 31.3 us
  blocking collectives: 18.7 us -> 0 us
  other arithmetic: 14.7 us -> 0 us
  between operations: 13.5 us -> 0.01 us
    all_gather x1 -> x0, waiting for transfers between devices: 42 us -> none  [per_device(): return lax.all_gather(zonal, 'lat', axis=2, tiled=True)]
    pallas_call x0 -> x1, Pallas kernels: none -> 31.3 us  [per_device(): pl.pallas_call(functools.partial(kernel, dims), out_shape=jax.ShapeDtypeS...]
    psum x1 -> x0, waiting for transfers between devices: 21 us -> none  [per_device(): totals, weight_total = lax.psum((row_sum, row_weight), 'lon')]
    psum x1 -> x0, blocking collectives: 12.6 us -> none  [per_device(): totals, weight_total = lax.psum((row_sum, row_weight), 'lon')]
    reduce_sum x2 -> x0, other arithmetic: 10.5 us -> none  [the longest x1 8.95 us: per_device(): row_sum = jnp.sum(fields.astype(jnp.float32) * joined[None], axis=-1)]
    all_gather x1 -> x0, blocking collectives: 6.14 us -> none  [per_device(): whole_half = lax.all_gather(half_own, 'lon', axis=1, tiled=True)]
    div x1 -> x0, other arithmetic: 1.6 us -> none  [per_device(): zonal = totals / weight_total[None]]
    unnamed x2 -> x1, local copies, waits for them, and re-layouts: 2.62 us -> 2.52 us
  transfers between devices with their start and end apart: 2 -> 0, of which waited for: 2 -> 0; matrix products, arithmetic and copies ran while one was open for 0% -> 0% of each run, Pallas kernels for 0% -> 0%
where the time goes in v1:
time: 34 us; the launch traced here: 33.9 us
  Pallas kernels  31.3 us (92%)
  local copies, waits for them, and re-layouts  2.52 us (7%)
    pallas_call x1, Pallas kernels, per_device(): pl.pallas_call(functools.partial(kernel, dims), out_shape=jax.ShapeDtypeS...  31.3 us
    unnamed x1, local copies, waits for them, and re-layouts  2.52 us

profile of v1, /device:TPU:0, one launch (start us, length us, event | category | flops | bytes accessed | tf_op | source)
XLA Modules:
  0.0 33.9 jit_solution(17113155480690650122)
XLA Ops:
  0.0 31.3 %shard_map.55 = f32[320,1024]{1,0:T(8,128)} custom-call(bf16[320,128,128]{2,1,0:T(8,128)(2,1)} %bitcast.4, f32[128,128]{1,0:T(8,128)} %area.1, s32[16,128,128]{2,1,0:T(8,128)} %ocean.1, s32[1,512]{1,0:T(1,128)} %bitcast.6, s32[1,512]{1,0:T(1,128)} %bitcast.7), custom_call_target="tpu_custom_call" | custom-call | tf_op jit(solution)/shard_map/pallas_call | solution.py:248
  31.3 2.5 %copy.7 = f32[20,16,1024]{2,1,0:T(8,128)} copy(f32[20,16,1024]{2,1,0:T(8,128)} %bitcast.5) | data formatting | bytes 2621440

commit v2 on v1

--- a/solution.py
+++ b/solution.py
@@ -9,18 +9,26 @@
 
 MESH = pl.DeviceIdType.MESH
 GROUP = 8
+PACK = 16
+TOP_CODE = 32767.0
+LEAST = 1e-33
+
+
+def step_of(exponent):
+    return jnp.exp2(exponent) * (1.0 / TOP_CODE)
 
 
 def kernel(
     dims, fields, area, ocean, partner, counted, out,
-    fv, av, ov, pv, cv, wt, wf, hb, part, recv,
+    fv, av, ov, pv, cv, wt, hb, part, recv,
     fsem, isem, hs, hr, ps, pr, zs, zr, x0s, x0r, y1s, y1r, y0s, y0r, x1s, x1r, ws, wr, cs, cr,
 ):
     n_lat, n_lon, nx, nz, ny, nc = dims
     levels, lat_rows, lon_cols = ocean.shape
     rows = fields.shape[0] // n_lon
     groups = rows // GROUP
-    first = (groups + 1) // 2 * GROUP
+    coded = out.shape[2]
+    first = (coded // PACK + 1) // 2 * PACK
     band, me = lax.axis_index("lat"), lax.axis_index("lon")
     z, x = band // nx, band % nx
     y, core = me // nc, me % nc
@@ -64,11 +72,23 @@
         pl.semaphore_signal(
             barrier, inc=1, device_id={"lat": lat_at(dz, dx), "lon": lon_at(dy, dc)}, device_id_type=MESH
         )
-    pl.semaphore_wait(barrier, len(greeted))
-
     for c in ins:
         c.wait()
     own_lanes = pl.ds(pl.multiple_of(me * lon_cols, lon_cols), lon_cols)
+
+    fold = jnp.logical_and(
+        lax.broadcasted_iota(jnp.int32, (lat_rows, lon_cols), 0) == lat_rows - 1, top
+    )
+    cell = (jnp.where(fold, cv[:, own_lanes].astype(jnp.float32), 1.0) * av[...]).T
+
+    def weigh(l, carry):
+        sea = ov[l].astype(jnp.float32).T
+        wt[l] = cell * sea
+        part[me, pl.ds(rows + l, 1), :] = jnp.sum(cell * (sea + 0.05), axis=0, keepdims=True)
+        return carry
+
+    lax.fori_loop(0, levels, weigh, 0, unroll=2)
+    pl.semaphore_wait(barrier, len(greeted))
 
     @pl.when(top)
     def _():
@@ -95,27 +115,14 @@
             whole, chosen, (((1,), (0,)), ((), ())),
             precision=lax.Precision.HIGHEST, preferred_element_type=jnp.float32,
         )
-        wf[...] = hb[me] + joined
+        filler = jnp.zeros((lon_cols - levels, lon_cols), jnp.float32)
+        column = jnp.concatenate([hb[me] + joined, filler], axis=0).T
+        last = lax.broadcasted_iota(jnp.int32, (lon_cols, lat_rows), 1) == lat_rows - 1
+        for l in range(levels):
+            wt[l] = jnp.where(last, column[:, l : l + 1], wt[l])
         for k, (dy, dc) in enumerate(targets):
             h_copy(k, dy, dc, me).wait_send()
 
-    @pl.when(jnp.logical_not(top))
-    def _():
-        wf[...] = jnp.zeros_like(wf)
-
-    fold = jnp.logical_and(
-        lax.broadcasted_iota(jnp.int32, (lat_rows, lon_cols), 0) == lat_rows - 1, top
-    )
-    cell = jnp.where(fold, cv[:, own_lanes].astype(jnp.float32), 1.0) * av[...]
-
-    def weigh(l, carry):
-        sea = ov[l].astype(jnp.float32)
-        weight = jnp.where(fold, wf[pl.ds(l, 1), :], cell * sea)
-        wt[l] = weight.T
-        part[me, pl.ds(rows + l, 1), :] = jnp.sum((cell * (sea + 0.05)).T, axis=0, keepdims=True)
-        return carry
-
-    lax.fori_loop(0, levels, weigh, 0)
     for dy, dc in targets:
         part[lon_at(dy, dc), rows:, :] = part[me, rows:, :]
 
@@ -153,23 +160,24 @@
     part[me, rows:, :] = total_weight
 
     def region(dz, dx, dy, dc, half):
-        start, size = ((0, rows), (0, first), (first, rows - first))[half]
-        return out.at[
-            pl.ds(pl.multiple_of(lon_at(dy, dc) * rows + start, GROUP), size),
-            pl.ds(pl.multiple_of(lat_at(dz, dx) * lat_rows, lat_rows), lat_rows),
-        ]
-
-    own_band = pl.ds(pl.multiple_of(band * lat_rows, lat_rows), lat_rows)
+        start, size = ((0, coded), (0, first), (first, coded - first))[half]
+        return out.at[lat_at(dz, dx), lon_at(dy, dc), pl.ds(start, size)]
+
+    means = []
     for g in range(groups):
         at = slice(g * GROUP, (g + 1) * GROUP)
         total = part[me, at, :]
         for s in slots:
             total += recv[s, at, :]
-        index = me * groups + g
-        base = pl.multiple_of((index * GROUP) % levels, GROUP)
-        out[pl.ds(pl.multiple_of(index * GROUP, GROUP), GROUP), own_band] = (
-            total / part[me, pl.ds(rows + base, GROUP), :]
-        )
+        base = pl.multiple_of(((me * groups + g) * GROUP) % levels, GROUP)
+        means.append(total / part[me, pl.ds(rows + base, GROUP), :])
+    mean = jnp.concatenate(means, axis=0)
+    largest = jnp.maximum(jnp.max(jnp.abs(mean), axis=0, keepdims=True), LEAST)
+    exponent = jnp.ceil(jnp.log2(largest) + 1e-4)
+    codes = jnp.round(mean / step_of(exponent))
+    tail = jnp.broadcast_to(exponent, (coded - rows, exponent.shape[1]))
+    block = jnp.concatenate([codes, tail], axis=0).astype(jnp.int32)
+    out[band, me] = block.astype(jnp.int16)
 
     sent = []
 
@@ -237,6 +245,13 @@
         p_copy(k, dy, dc, lon_at(dy, dc), me).wait_send()
 
 
+def decode(codes, out):
+    n_lon, rows = codes.shape[1], out.shape[0] // codes.shape[1]
+    for q in range(n_lon):
+        block = codes[0, q].astype(jnp.int32).astype(jnp.float32)
+        out[q * rows : (q + 1) * rows, :] = block[:rows] * step_of(block[rows : rows + 1])
+
+
 def per_device(dims, fields, area, ocean, partner, counted):
     n_lat, n_lon, nx, nz, ny, nc = dims
     count, levels, lat_rows, lon_cols = fields.shape
@@ -245,9 +260,10 @@
     hands = nz * (1 + (nx - 1) + (ny - 1) + 2 * (nx - 1) * (ny - 1)) * max(nc - 1, 1)
     dma = pltpu.SemaphoreType.DMA
     any_space = pl.BlockSpec(memory_space=pl.ANY)
-    zonal = pl.pallas_call(
+    coded = (rows + PACK) // PACK * PACK
+    codes = pl.pallas_call(
         functools.partial(kernel, dims),
-        out_shape=jax.ShapeDtypeStruct((total, n_lat * lat_rows), jnp.float32),
+        out_shape=jax.ShapeDtypeStruct((n_lat, n_lon, coded, lat_rows), jnp.int16),
         in_specs=[any_space] * 5,
         out_specs=pl.BlockSpec(memory_space=pltpu.VMEM),
         scratch_shapes=[
@@ -257,7 +273,6 @@
             pltpu.VMEM((1, n_lon * lon_cols), jnp.int32),
             pltpu.VMEM((1, n_lon * lon_cols), jnp.int32),
             pltpu.VMEM((levels, lon_cols, lat_rows), jnp.float32),
-            pltpu.VMEM((levels, lon_cols), jnp.float32),
             pltpu.VMEM((n_lon, levels, lon_cols), jnp.float32),
             pltpu.VMEM((n_lon, rows + levels, lat_rows), jnp.float32),
             pltpu.VMEM((n_lon, rows + levels, lat_rows), jnp.float32),
@@ -278,6 +293,13 @@
         fields.reshape(total, lat_rows, lon_cols), area, ocean,
         partner.reshape(1, -1), counted.reshape(1, -1),
     )
+    zonal = pl.pallas_call(
+        decode,
+        grid=(n_lat,),
+        out_shape=jax.ShapeDtypeStruct((total, n_lat * lat_rows), jnp.float32),
+        in_specs=[pl.BlockSpec((1, n_lon, coded, lat_rows), lambda b: (b, 0, 0, 0))],
+        out_specs=pl.BlockSpec((total, lat_rows), lambda b: (0, b)),
+    )(codes)
     return zonal.reshape(count, levels, n_lat * lat_rows)
 
 

time: 34 us -> 34.9 us (1.026)
  Pallas kernels: 31.3 us -> 34.6 us
  local copies, waits for them, and re-layouts: 2.52 us -> 0 us
    pallas_call x0 -> x1, Pallas kernels: none -> 5.2 us  [per_device(): pl.pallas_call(decode, grid=(n_lat,), out_shape=jax.ShapeDtypeStruct((tot...]
    unnamed x1 -> x0, local copies, waits for them, and re-layouts: 2.52 us -> none
    pallas_call x1, Pallas kernels: 31.3 us -> 29.4 us  [per_device(): pl.pallas_call(functools.partial(kernel, dims), out_shape=jax.ShapeDtypeS...]
where the time goes in v2:
time: 34.9 us; the launch traced here: 34.6 us
  Pallas kernels  34.6 us (99%)
    pallas_call x1, Pallas kernels, per_device(): pl.pallas_call(functools.partial(kernel, dims), out_shape=jax.ShapeDtypeS...  29.4 us
    pallas_call x1, Pallas kernels, per_device(): pl.pallas_call(decode, grid=(n_lat,), out_shape=jax.ShapeDtypeStruct((tot...  5.2 us

profile of v2, /device:TPU:0, one launch (start us, length us, event | category | flops | bytes accessed | tf_op | source)
XLA Modules:
  0.0 34.6 jit_solution(12868814661754931501)
XLA Ops:
  0.0 29.4 %shard_map.55.codes = s16[8,4,96,128]{3,2,1,0:T(8,128)(2,1)} custom-call(bf16[320,128,128]{2,1,0:T(8,128)(2,1)} %bitcast.4, f32[128,128]{1,0:T(8,128)} %area.1, s32[16,128,128]{2,1,0:T(8,128)} %ocean.1, s32[1,512]{1,0:T(1,128)} %bitcast.5, s32[1,512]{1,0:T(1,128)} %bitcast.6), custom_call_target="tpu_custom_call" | custom-call | tf_op jit(solution)/shard_map/pallas_call | solution.py:264
  29.4 5.2 %shard_map.56 = f32[320,1024]{1,0:T(8,128)} custom-call(s16[8,4,96,128]{3,2,1,0:T(8,128)(2,1)} %shard_map.55.codes), custom_call_target="tpu_custom_call" | custom-call | tf_op jit(solution)/shard_map/pallas_call | solution.py:296

commit v3 on v2

--- a/solution.py
+++ b/solution.py
@@ -246,10 +246,14 @@
 
 
 def decode(codes, out):
-    n_lon, rows = codes.shape[1], out.shape[0] // codes.shape[1]
-    for q in range(n_lon):
-        block = codes[0, q].astype(jnp.int32).astype(jnp.float32)
-        out[q * rows : (q + 1) * rows, :] = block[:rows] * step_of(block[rows : rows + 1])
+    n_lat, n_lon, coded, lat_rows = codes.shape
+    rows = out.shape[0] // n_lon
+    for b in range(n_lat):
+        for q in range(n_lon):
+            block = codes[b, q].astype(jnp.int32).astype(jnp.float32)
+            out[q * rows : (q + 1) * rows, b * lat_rows : (b + 1) * lat_rows] = (
+                block[:rows] * step_of(block[rows : rows + 1])
+            )
 
 
 def per_device(dims, fields, area, ocean, partner, counted):
@@ -295,10 +299,9 @@
     )
     zonal = pl.pallas_call(
         decode,
-        grid=(n_lat,),
         out_shape=jax.ShapeDtypeStruct((total, n_lat * lat_rows), jnp.float32),
-        in_specs=[pl.BlockSpec((1, n_lon, coded, lat_rows), lambda b: (b, 0, 0, 0))],
-        out_specs=pl.BlockSpec((total, lat_rows), lambda b: (0, b)),
+        in_specs=[pl.BlockSpec(memory_space=pltpu.VMEM)],
+        out_specs=pl.BlockSpec(memory_space=pltpu.VMEM),
     )(codes)
     return zonal.reshape(count, levels, n_lat * lat_rows)
 

time: 34.9 us -> 32 us (0.917)
  Pallas kernels: 34.6 us -> 31.8 us
    pallas_call x1, Pallas kernels: 5.2 us -> 2.39 us  [per_device(): pl.pallas_call(decode, out_shape=jax.ShapeDtypeStruct((total, n_lat * lat...]
where the time goes in v3:
time: 32 us; the launch traced here: 31.8 us
  Pallas kernels  31.8 us (99%)
    pallas_call x1, Pallas kernels, per_device(): pl.pallas_call(functools.partial(kernel, dims), out_shape=jax.ShapeDtypeS...  29.4 us
    pallas_call x1, Pallas kernels, per_device(): pl.pallas_call(decode, out_shape=jax.ShapeDtypeStruct((total, n_lat * lat...  2.39 us

profile of v3, /device:TPU:0, one launch (start us, length us, event | category | flops | bytes accessed | tf_op | source)
XLA Modules:
  0.0 31.8 jit_solution(18381440579929596884)
XLA Ops:
  0.0 29.4 %shard_map.55.codes = s16[8,4,96,128]{3,2,1,0:T(8,128)(2,1)} custom-call(bf16[320,128,128]{2,1,0:T(8,128)(2,1)} %bitcast.4, f32[128,128]{1,0:T(8,128)} %area.1, s32[16,128,128]{2,1,0:T(8,128)} %ocean.1, s32[1,512]{1,0:T(1,128)} %bitcast.5, s32[1,512]{1,0:T(1,128)} %bitcast.6), custom_call_target="tpu_custom_call" | custom-call | tf_op jit(solution)/shard_map/pallas_call | solution.py:268
  29.4 2.4 %shard_map.56 = f32[320,1024]{1,0:T(8,128)} custom-call(s16[8,4,96,128]{3,2,1,0:T(8,128)(2,1)} %shard_map.55.codes), custom_call_target="tpu_custom_call" | custom-call | tf_op jit(solution)/shard_map/pallas_call | solution.py:300
